TPU v7x, 32 devices: a 4x4x1 block of a 4x4x8 slice. The times are simulated.
32 devices in a mesh: dp: 1 (over z), tp: 4 (over y), sp: 8 (over x, core).
Axes of the slice: x: 4, y: 4, z: 1, core: 2. Of those that a mesh axis runs over, the one named last changes fastest.
The devices are a block of a 4x4x8 slice.
Arguments:
- k_cache: bfloat16 [4, 8, 4, 8192, 64], P(None, 'dp', 'tp', 'sp')
- v_cache: bfloat16 [4, 8, 4, 8192, 64], P(None, 'dp', 'tp', 'sp')
- lengths: int32 [8], P('dp')
- hidden: bfloat16 [8, 2048], P(('dp', 'sp'))
- ln_gain: bfloat16 [4, 2048], replicated
- w_query: bfloat16 [4, 2048, 2048], P(None, None, 'tp')
- w_key: bfloat16 [4, 2048, 256], P(None, None, 'tp')
- w_value: bfloat16 [4, 2048, 256], P(None, None, 'tp')
- w_out: bfloat16 [4, 2048, 2048], P(None, 'tp')
- w_gate: bfloat16 [4, 2048, 5632], P(None, None, 'tp')
- w_up: bfloat16 [4, 2048, 5632], P(None, None, 'tp')
- w_down: bfloat16 [4, 5632, 2048], P(None, 'tp')
Outputs:
- output 1: bfloat16 [8, 2048], P(('dp', 'sp'))
- output 2: bfloat16 [3, 8, 4, 4096, 64], P(None, ('dp', 'sp'), 'tp')
- output 3: bfloat16 [3, 8, 4, 4096, 64], P(None, ('dp', 'sp'), 'tp')
- output 4: bfloat16 [8, 4, 8192, 64], P(('dp', 'sp'), 'tp')
- output 5: bfloat16 [8, 4, 8192, 64], P(('dp', 'sp'), 'tp')
All inputs are finite; a program needn't handle non-finite values.
Results may differ from a plain program's by a relative error of at most 0.02.
Values are sent between devices in bfloat16 or wider.
A program may use at most 768 MiB of HBM per device.

v0:
```python
import jax
import jax.numpy as jnp
from jax import lax
from jax.sharding import PartitionSpec as P, NamedSharding

WINDOW = 4096
ROPE_BASE = 50000
NORM_EPS = 1e-5


def layer_norm(rows_in, gain):
    rows32 = rows_in.astype(jnp.float32)
    centered = rows32 - rows32.mean(axis=-1, keepdims=True)
    variance = (centered * centered).mean(axis=-1, keepdims=True)
    scaled = centered * lax.rsqrt(variance + NORM_EPS)
    return (scaled * gain.astype(jnp.float32)).astype(jnp.bfloat16)


def rotary(proj, positions, head_dim):
    half_dim = head_dim // 2
    inv_freq = 1.0 / (ROPE_BASE ** (jnp.arange(half_dim, dtype=jnp.float32) * 2.0 / head_dim))
    angles = positions.astype(jnp.float32)[:, None] * inv_freq[None, :]
    cosine = jnp.cos(angles)[:, None, :]
    sine = jnp.sin(angles)[:, None, :]
    heads = proj.reshape(proj.shape[0], -1, head_dim)
    first = heads[..., :half_dim]
    second = heads[..., half_dim:]
    turned = jnp.concatenate([first * cosine - second * sine, second * cosine + first * sine], axis=-1)
    return turned.reshape(proj.shape)


def project(normed, w_query_l, w_key_l, w_value_l, positions, head_dim, sliding):
    n_rows = normed.shape[0]
    query = jnp.dot(normed, w_query_l, preferred_element_type=jnp.float32)
    key_new = jnp.dot(normed, w_key_l, preferred_element_type=jnp.float32)
    value_new = jnp.dot(normed, w_value_l, preferred_element_type=jnp.float32)
    if sliding:
        query = rotary(query, positions, head_dim)
        key_new = rotary(key_new, positions, head_dim)
    query = query.astype(jnp.bfloat16).reshape(n_rows, -1, head_dim)
    key_new = key_new.astype(jnp.bfloat16).reshape(n_rows, -1, 1, head_dim)
    value_new = value_new.astype(jnp.bfloat16).reshape(n_rows, -1, 1, head_dim)
    return query, key_new, value_new


def mlp_part(normed, w_gate_l, w_up_l, w_down_l):
    gate_proj = jnp.dot(normed, w_gate_l, preferred_element_type=jnp.float32)
    up_proj = jnp.dot(normed, w_up_l, preferred_element_type=jnp.float32)
    activated = (jax.nn.silu(gate_proj) * up_proj).astype(jnp.bfloat16)
    return jnp.dot(activated, w_down_l, preferred_element_type=jnp.float32)


def attend_local(query, keys, values, key_valid):
    n_rows, n_heads, head_dim = query.shape
    kv_local = keys.shape[1]
    grouped = query.reshape(n_rows, kv_local, n_heads // kv_local, head_dim)
    scores = jnp.einsum("bkgd,bksd->bkgs", grouped, keys, preferred_element_type=jnp.float32) * head_dim ** -0.5
    if key_valid is not None:
        scores = jnp.where(key_valid[:, None, None, :], scores, -1e30)
    weights = jax.nn.softmax(scores, axis=-1).astype(jnp.bfloat16)
    mixed = jnp.einsum("bkgs,bksd->bkgd", weights, values, preferred_element_type=jnp.float32)
    return mixed.astype(jnp.bfloat16).reshape(n_rows, n_heads * head_dim)


def place_new(window_rows, row_lengths, new_entry):
    slot_ids = jnp.arange(window_rows.shape[2], dtype=jnp.int32)
    is_new = (slot_ids[None, :] == (row_lengths % WINDOW)[:, None])[:, None, :, None]
    return jnp.where(is_new, new_entry, window_rows)


def window_from_rows(seq_rows, row_lengths, new_entry):
    n_rows, kv_local, seq_len, head_dim = seq_rows.shape
    folds = seq_len // WINDOW
    positions = jnp.arange(seq_len, dtype=jnp.int32).reshape(folds, WINDOW)
    row_last = row_lengths[:, None, None]
    in_window = (positions[None] > row_last - WINDOW) & (positions[None] < row_last)
    folded = seq_rows.reshape(n_rows, kv_local, folds, WINDOW, head_dim)
    window_rows = jnp.where(in_window[:, None, :, :, None], folded, 0).sum(axis=2)
    return place_new(window_rows, row_lengths, new_entry)


def global_from_rows(seq_rows, row_lengths, new_entry):
    positions = jnp.arange(seq_rows.shape[2], dtype=jnp.int32)[None, :]
    row_last = row_lengths[:, None]
    kept = jnp.where((positions < row_last)[:, None, :, None], seq_rows, 0)
    return jnp.where((positions == row_last)[:, None, :, None], new_entry, kept)


def solution(mesh):
    cache_spec = P(None, "dp", "tp", "sp", None)
    row_spec = P(("dp", "sp"), None)
    col_spec = P(None, None, "tp")
    inner_spec = P(None, "tp", None)
    window_spec = P(None, ("dp", "sp"), "tp", None, None)
    global_spec = P(("dp", "sp"), "tp", None, None)
    in_specs = (cache_spec, cache_spec, P("dp"), row_spec, P(None, None), col_spec, col_spec, col_spec, inner_spec, col_spec, col_spec, inner_spec)
    out_specs = (row_spec, window_spec, window_spec, global_spec, global_spec)

    def device_step(k_cache, v_cache, lengths, hidden, ln_gain, w_query, w_key, w_value, w_out, w_gate, w_up, w_down):
        n_layers = w_query.shape[0]
        rows_dev = hidden.shape[0]
        head_dim = k_cache.shape[-1]
        row_start = lax.axis_index("sp") * rows_dev
        my_lengths = lax.dynamic_slice_in_dim(lengths, row_start, rows_dev)
        residual = hidden
        windows_k = []
        windows_v = []
        for layer in range(n_layers):
            sliding = layer < n_layers - 1
            full_k = lax.all_gather(k_cache[layer], "sp", axis=2, tiled=True)
            full_v = lax.all_gather(v_cache[layer], "sp", axis=2, tiled=True)
            own_k = lax.dynamic_slice_in_dim(full_k, row_start, rows_dev, axis=0)
            own_v = lax.dynamic_slice_in_dim(full_v, row_start, rows_dev, axis=0)
            normed = layer_norm(residual, ln_gain[layer])
            query, key_new, value_new = project(normed, w_query[layer], w_key[layer], w_value[layer], my_lengths, head_dim, sliding)
            if sliding:
                keys = window_from_rows(own_k, my_lengths, key_new)
                values = window_from_rows(own_v, my_lengths, value_new)
                windows_k.append(keys)
                windows_v.append(values)
                key_valid = None
            else:
                keys = global_from_rows(own_k, my_lengths, key_new)
                values = global_from_rows(own_v, my_lengths, value_new)
                key_valid = jnp.arange(keys.shape[2], dtype=jnp.int32)[None, :] <= my_lengths[:, None]
            mixed = attend_local(query, keys, values, key_valid)
            attn_out = lax.psum(jnp.dot(mixed, w_out[layer], preferred_element_type=jnp.float32), "tp")
            mlp_out = lax.psum(mlp_part(normed, w_gate[layer], w_up[layer], w_down[layer]), "tp")
            residual = (residual.astype(jnp.float32) + attn_out + mlp_out).astype(jnp.bfloat16)
        return residual, jnp.stack(windows_k), jnp.stack(windows_v), keys, values

    return jax.shard_map(device_step, mesh=mesh, in_specs=in_specs, out_specs=out_specs, check_vma=False)
```

profile of v0, /device:TPU:96, one launch (start us, length us, event | category | flops | bytes accessed | tf_op | source)
XLA Modules:
  0.0 470.0 jit_solution(13553870793792818080)
XLA Ops:
  7.2 4.4 fusion.203
  11.8 4.3 fusion.204
  30.3 5.7 %fusion.202 = (bf16[1,2048,512]{2,1,0:T(8,128)(2,1)}, bf16[1,2048,512]{2,1,0:T(8,128)(2,1)}, bf16[1,2048,512]{2,1,0:T(8,128)(2,1)}) fusion(bf16[4,2048,512]{2,1,0:T(8,128)(2,1)} %param.17), kind=kLoop, calls=%fused_computation.278 | loop fusion | bytes 12582912 | tf_op jit(solution)/shard_map/slice | solution.py:115
  40.9 3.7 fusion.52
  44.6 3.5 fusion.55
  57.3 4.1 all-gather.17.cloned.1.call-done
  65.4 44.7 %all-gather.19.cloned.1.call-done = bf16[1,8,1,8192,64]{3,4,2,1,0:T(8,128)(2,1)} async-done(((bf16[1,8,1,1024,64]{3,4,2,1,0:T(8,128)(2,1)}), bf16[1,8,1,8192,64]{3,4,2,1,0:T(8,128)(2,1)}) %all-gather.19.cloned.1.call-update) | async-done | bytes 8388624 | tf_op jit(solution)/shard_map/all_gather | solution.py:111
  115.0 44.5 %all-gather.21.cloned.1.call-done = bf16[1,8,1,8192,64]{3,4,2,1,0:T(8,128)(2,1)} async-done(((bf16[1,8,1,1024,64]{3,4,2,1,0:T(8,128)(2,1)}), bf16[1,8,1,8192,64]{3,4,2,1,0:T(8,128)(2,1)}) %all-gather.21.cloned.1.call-update) | async-done | bytes 8388624 | tf_op jit(solution)/shard_map/all_gather | solution.py:110
  164.4 43.8 %all-gather.23.cloned.1.call-done = bf16[1,8,1,8192,64]{3,4,2,1,0:T(8,128)(2,1)} async-done(((bf16[1,8,1,1024,64]{3,4,2,1,0:T(8,128)(2,1)}), bf16[1,8,1,8192,64]{3,4,2,1,0:T(8,128)(2,1)}) %all-gather.23.cloned.1.call-update) | async-done | bytes 8388624 | tf_op jit(solution)/shard_map/all_gather | solution.py:111
  213.1 44.3 %all-gather.25.cloned.1.call-done = bf16[1,8,1,8192,64]{3,4,2,1,0:T(8,128)(2,1)} async-done(((bf16[1,8,1,1024,64]{3,4,2,1,0:T(8,128)(2,1)}), bf16[1,8,1,8192,64]{3,4,2,1,0:T(8,128)(2,1)}) %all-gather.25.cloned.1.call-update) | async-done | bytes 8388624 | tf_op jit(solution)/shard_map/all_gather | solution.py:110
  262.3 43.8 %all-gather.27.cloned.1.call-done = bf16[1,8,1,8192,64]{3,4,2,1,0:T(8,128)(2,1)} async-done(((bf16[1,8,1,1024,64]{3,4,2,1,0:T(8,128)(2,1)}), bf16[1,8,1,8192,64]{3,4,2,1,0:T(8,128)(2,1)}) %all-gather.27.cloned.1.call-update) | async-done | bytes 8388624 | tf_op jit(solution)/shard_map/all_gather | solution.py:111
  311.0 16.0 %fusion.85 = (bf16[4096,64]{0,1:T(8,128)(2,1)}, bf16[4096,64]{0,1:T(8,128)(2,1)S(1)}, bf16[4096,64]{0,1:T(8,128)(2,1)}, bf16[4096,64]{0,1:T(8,128)(2,1)}, bf16[4...) fusion(bf16[1,1,2,4096,64]{3,2,4,1,0:T(2,128)(2,1)} %reshape.1202, pred[2,4096]{1,0:T(4,128)(4,1)S(1)} %compare_and_fusion, ...), kind=kLoop, calls=%fused_computation.93 | loop fusion | flops 4718592 | bytes 9445376 | tf_op jit(solution)/shard_map/reduce_sum | solution.py:78
  330.8 17.0 %all-reduce.3 = (f32[1,2048]{1,0:T(1,128)S(1)}, f32[1,2048]{1,0:T(1,128)S(1)}) all-reduce(f32[1,2048]{1,0:T(1,128)S(1)} %fusion.19, f32[1,2048]{1,0:T(1,128)S(1)} %fusion.45), channel_id=1, replica_groups=mesh['dp'=1,'tp'=4,'sp'=8] {'tp'}, use_global_device_ids=true, to_apply=%region_7.8 | all-reduce | flops 4096 | bytes 32768 | tf_op jit(solution)/shard_map/psum | solution.py:128
  356.4 3.5 fusion.58
  359.9 3.5 fusion.61
  365.5 3.5 fusion.13
  369.0 14.6 %all-reduce.2 = (f32[1,2048]{1,0:T(1,128)S(1)}, f32[1,2048]{1,0:T(1,128)S(1)}) all-reduce(f32[1,2048]{1,0:T(1,128)S(1)} %fusion.13, f32[1,2048]{1,0:T(1,128)S(1)} %fusion.43), channel_id=1, replica_groups=mesh['dp'=1,'tp'=4,'sp'=8] {'tp'}, use_global_device_ids=true, to_apply=%region_15.16 | all-reduce | flops 4096 | bytes 32768 | tf_op jit(solution)/shard_map/psum | solution.py:128
  391.6 3.5 fusion.64
  395.2 3.5 fusion.67
  400.7 3.5 fusion.7
  404.2 15.2 %all-reduce.1 = (f32[1,2048]{1,0:T(1,128)S(1)}, f32[1,2048]{1,0:T(1,128)S(1)}) all-reduce(f32[1,2048]{1,0:T(1,128)S(1)} %fusion.7, f32[1,2048]{1,0:T(1,128)S(1)} %fusion.41), channel_id=1, replica_groups=mesh['dp'=1,'tp'=4,'sp'=8] {'tp'}, use_global_device_ids=true, to_apply=%region_23.24 | all-reduce | flops 4096 | bytes 32768 | tf_op jit(solution)/shard_map/psum | solution.py:128
  426.4 3.6 fusion.70
  430.0 3.5 fusion.73
  444.1 14.6 %all-reduce = (f32[1,2048]{1,0:T(1,128)S(1)}, f32[1,2048]{1,0:T(1,128)S(1)}) all-reduce(f32[1,2048]{1,0:T(1,128)S(1)} %fusion.1, f32[1,2048]{1,0:T(1,128)S(1)} %fusion.37), channel_id=1, replica_groups=mesh['dp'=1,'tp'=4,'sp'=8] {'tp'}, use_global_device_ids=true, to_apply=%region_29.30 | all-reduce | flops 4096 | bytes 32768 | tf_op jit(solution)/shard_map/psum | solution.py:128
  (139 shorter events, 94.5 us)
Async XLA Ops:
  7.2 54.2 %all-gather.17.cloned.1.call-start = ((), (), s32[]{:S(2)}) async-start(), calls=%async_computation | async-start | bytes 9437184 | tf_op jit(solution)/shard_map/all_gather | solution.py:110
  11.7 98.5 %all-gather.19.cloned.1.call-start = ((), (), s32[]{:S(2)}) async-start(), calls=%async_computation.1 | async-start | bytes 9437184 | tf_op jit(solution)/shard_map/all_gather | solution.py:111
  16.1 4.4 copy-start.16
  16.1 10.3 %copy-start.15 = (bf16[1,2048]{1,0:T(2,128)(2,1)S(1)}, bf16[1,2048]{1,0:T(2,128)(2,1)}, u32[]{:S(2)}) copy-start(bf16[1,2048]{1,0:T(2,128)(2,1)} %param.15) | copy-start | bytes 12292
  16.1 12.9 %copy-start.13 = (bf16[4,2048]{1,0:T(4,128)(2,1)S(1)}, bf16[4,2048]{1,0:T(4,128)(2,1)}, u32[]{:S(2)}) copy-start(bf16[4,2048]{1,0:T(4,128)(2,1)} %param.16) | copy-start | bytes 49156
  16.2 143.4 %all-gather.21.cloned.1.call-start = ((), (), s32[]{:S(2)}) async-start(), calls=%async_computation.2 | async-start | bytes 9437184 | tf_op jit(solution)/shard_map/all_gather | solution.py:110
  17.0 191.3 %all-gather.23.cloned.1.call-start = ((), (), s32[]{:S(2)}) async-start(), calls=%async_computation.3 | async-start | bytes 9437184 | tf_op jit(solution)/shard_map/all_gather | solution.py:111
  17.6 239.9 %all-gather.25.cloned.1.call-start = ((), (), s32[]{:S(2)}) async-start(), calls=%async_computation.4 | async-start | bytes 9437184 | tf_op jit(solution)/shard_map/all_gather | solution.py:110
  18.2 287.9 %all-gather.27.cloned.1.call-start = ((), (), s32[]{:S(2)}) async-start(), calls=%async_computation.5 | async-start | bytes 9437184 | tf_op jit(solution)/shard_map/all_gather | solution.py:111
  18.9 416.2 %all-gather.29.cloned.1.call-start = ((), (), s32[]{:S(2)}) async-start(), calls=%async_computation.6 | async-start | bytes 9437184 | tf_op jit(solution)/shard_map/all_gather | solution.py:110
  19.7 415.4 %all-gather.31.cloned.1.call-start = ((), (), s32[]{:S(2)}) async-start(), calls=%async_computation.7 | async-start | bytes 9437184 | tf_op jit(solution)/shard_map/all_gather | solution.py:111
  40.9 7.2 %copy-start = (bf16[1,2048,512]{2,1,0:T(8,128)(2,1)S(1)}, bf16[1,2048,512]{2,1,0:T(8,128)(2,1)}, u32[]{:S(2)}) copy-start(bf16[1,2048,512]{2,1,0:T(8,128)(2,1)} %get-tuple-element.26) | copy-start | bytes 6291460
  327.0 1.4 copy-start.3
  327.0 27.2 %copy-start.5 = (bf16[4096,64]{0,1:T(8,128)(2,1)S(1)}, bf16[4096,64]{0,1:T(8,128)(2,1)}, u32[]{:S(2)}) copy-start(bf16[4096,64]{0,1:T(8,128)(2,1)} %get-tuple-element.7) | copy-start | bytes 1572868
  327.0 28.9 %copy-start.6 = (bf16[4096,64]{0,1:T(8,128)(2,1)S(1)}, bf16[4096,64]{0,1:T(8,128)(2,1)}, u32[]{:S(2)}) copy-start(bf16[4096,64]{0,1:T(8,128)(2,1)} %get-tuple-element.8) | copy-start | bytes 1572868
  363.4 25.0 %copy-start.2 = (bf16[4096,64]{0,1:T(8,128)(2,1)S(1)}, bf16[4096,64]{0,1:T(8,128)(2,1)}, u32[]{:S(2)}) copy-start(bf16[4096,64]{0,1:T(8,128)(2,1)} %get-tuple-element.5) | copy-start | bytes 1572868
  426.3 7.2 %copy-start.4 = (bf16[4096,64]{0,1:T(8,128)(2,1)S(1)}, bf16[4096,64]{0,1:T(8,128)(2,1)}, u32[]{:S(2)}) copy-start(bf16[4096,64]{0,1:T(8,128)(2,1)} %copy-done.3) | copy-start | bytes 1572868
  426.3 7.2 %copy-start.7 = (bf16[4096,64]{0,1:T(8,128)(2,1)S(1)}, bf16[4096,64]{0,1:T(8,128)(2,1)}, u32[]{:S(2)}) copy-start(bf16[4096,64]{0,1:T(8,128)(2,1)} %get-tuple-element.8) | copy-start | bytes 1572868
  426.3 7.2 %copy-start.8 = (bf16[4096,64]{0,1:T(8,128)(2,1)S(1)}, bf16[4096,64]{0,1:T(8,128)(2,1)}, u32[]{:S(2)}) copy-start(bf16[4096,64]{0,1:T(8,128)(2,1)} %get-tuple-element.9) | copy-start | bytes 1572868
  426.3 7.2 %copy-start.10 = (bf16[4096,64]{0,1:T(8,128)(2,1)S(1)}, bf16[4096,64]{0,1:T(8,128)(2,1)}, u32[]{:S(2)}) copy-start(bf16[4096,64]{0,1:T(8,128)(2,1)} %copy-done.9) | copy-start | bytes 1572868
  437.1 1.0 copy-start.14
  437.1 24.7 %copy-start.1 = (bf16[1,1,8192,64]{2,3,1,0:T(8,128)(2,1)}, bf16[1,1,8192,64]{2,3,1,0:T(8,128)(2,1)S(1)}, u32[]{:S(2)}) copy-start(bf16[1,1,8192,64]{2,3,1,0:T(8,128)(2,1)S(1)} %get-tuple-element.36) | copy-start | bytes 3145732
  437.1 22.2 %copy-start.12 = (bf16[1,1,1,4096,64]{3,4,2,1,0:T(8,128)(2,1)S(1)}, bf16[1,1,1,4096,64]{3,4,2,1,0:T(8,128)(2,1)}, u32[]{:S(2)}) copy-start(bf16[1,1,1,4096,64]{3,4,2,1,0:T(8,128)(2,1)} %get-tuple-element.44) | copy-start | bytes 1572868
  438.5 23.3 %copy-start.11 = (bf16[1,1,1,4096,64]{3,4,2,1,0:T(8,128)(2,1)S(1)}, bf16[1,1,1,4096,64]{3,4,2,1,0:T(8,128)(2,1)}, u32[]{:S(2)}) copy-start(bf16[1,1,1,4096,64]{3,4,2,1,0:T(8,128)(2,1)} %get-tuple-element.49) | copy-start | bytes 1572868
  (1 other events, 0.8 us)
Sparse Core Ops, SparseCore 0:
  11.8 49.4 all-gather.16
  62.9 47.1 all-gather.18
  112.3 47.1 all-gather.20
  161.0 47.1 all-gather.22
  210.2 47.1 all-gather.24
  258.9 47.1 all-gather.26
  308.3 47.2 all-gather.28
  357.2 47.1 all-gather.30
where the time goes:
time: 472 us; the launch traced here: 470 us
  waiting for transfers between devices  229 us (49%)
  matrix products  69.6 us (15%)
  blocking collectives  61.3 us (13%)
  local copies, waits for them, and re-layouts  53.5 us (11%)
  other arithmetic  32.7 us (7%)
  between operations  23.2 us (5%)
    all_gather x4, waiting for transfers between devices, device_step(): full_v = lax.all_gather(v_cache[layer], 'sp', axis=2, tiled=True)  132 us
    all_gather x4, waiting for transfers between devices, device_step(): full_k = lax.all_gather(k_cache[layer], 'sp', axis=2, tiled=True)  92.9 us
    psum x4, blocking collectives, device_step(): lax.psum(mlp_part(normed, w_gate[layer], w_up[layer], w_down[layer]), 'tp')  61.3 us
    reduce_sum x1, other arithmetic, window_from_rows(): jnp.where(in_window[:, None, :, :, None], folded, 0).sum(axis=2)  16 us
    reshape x6, local copies, waits for them, and re-layouts, window_from_rows(): folded = seq_rows.reshape(n_rows, kv_local, folds, WINDOW, head_dim)  14.9 us
    dot_general x4, matrix products, mlp_part(): gate_proj = jnp.dot(normed, w_gate_l, preferred_element_type=jnp.float32)  14.3 us
    dot_general x4, matrix products, mlp_part(): up_proj = jnp.dot(normed, w_up_l, preferred_element_type=jnp.float32)  14 us
    dot_general x4, matrix products, mlp_part(): return jnp.dot(activated, w_down_l, preferred_element_type=jnp.float32)  14 us
  transfers between devices with their start and end apart: 8, of which 6 were waited for; matrix products, arithmetic and copies ran while one was open for 29% of the time, Pallas kernels for 0%

commit v1 on v0

v1 whole, which is shorter than its diff:
```python
import functools

import jax
import jax.numpy as jnp
import numpy as np
from jax import lax
from jax.experimental import pallas as pl
from jax.experimental.pallas import tpu as pltpu
from jax.sharding import PartitionSpec as P

WINDOW = 4096
ROPE_BASE = 50000
NORM_EPS = 1e-5
LANES = 128
SUBLANES = 8
TILE = 256
F32 = jnp.float32
BF16 = jnp.bfloat16
MESH = pl.DeviceIdType.MESH


def contract_lanes(left, right):
    return lax.dot_general(left, right, (((1,), (1,)), ((), ())), preferred_element_type=F32)


def row_of(values, index):
    rows = lax.broadcasted_iota(jnp.int32, values.shape, 0)
    return jnp.where(rows == index, values, jnp.zeros_like(values))


def decode_kernel(n_sp, n_tp, len_ref, hid_ref, gain_ref, freq_row_ref, freq_col_ref, k_ref, v_ref, wq_ref, wk_ref, wv_ref, wo_ref, wg_ref, wu_ref, wd_ref,
                  hid_out, win_k_out, win_v_out, glob_k_out, glob_v_out,
                  stage, wq, wk, wv, wo, wg, wu, wd, win, glob, normed, query, act, total, sums,
                  send_sem, recv_sem, own_sem, weight_sem, out_sem, sum_send_sem, sum_recv_sem):
    n_layers = wq_ref.shape[0]
    piece = k_ref.shape[-1]
    head_dim = k_ref.shape[-2]
    q_width = wq_ref.shape[-1]
    ffn = wg_ref.shape[-1]
    dim = wq_ref.shape[1]
    n_heads = q_width // head_dim
    half = head_dim // 2
    blocks = dim // LANES
    n_low = WINDOW // piece
    me = lax.axis_index("sp")
    my_tp = lax.axis_index("tp")

    weight_pairs = ((wq_ref, wq), (wk_ref, wk), (wv_ref, wv), (wg_ref, wg), (wu_ref, wu), (wd_ref, wd), (wo_ref, wo))

    def weight_copies(layer):
        slot = layer % 2
        return [pltpu.make_async_copy(src.at[layer], dst.at[slot], weight_sem.at[slot, i]) for i, (src, dst) in enumerate(weight_pairs)]

    for copy in weight_copies(0):
        copy.start()

    barrier = pltpu.get_barrier_semaphore()
    for step in range(1, n_sp):
        pl.semaphore_signal(barrier, inc=1, device_id={"sp": lax.rem(me + step, n_sp)}, device_id_type=MESH)
    for step in range(1, n_tp):
        pl.semaphore_signal(barrier, inc=1, device_id={"tp": lax.rem(my_tp + step, n_tp)}, device_id_type=MESH)
    pl.semaphore_wait(barrier, n_sp + n_tp - 2)

    def sends(layer, kv):
        src = k_ref if kv == 0 else v_ref
        found = []
        for step in range(1, n_sp):
            dst = lax.rem(me + step, n_sp)
            found.append(pltpu.make_async_remote_copy(
                src_ref=src.at[layer, dst], dst_ref=stage.at[layer, kv, me],
                send_sem=send_sem.at[layer, kv, step], recv_sem=recv_sem.at[layer, kv, step],
                device_id={"sp": dst}, device_id_type=MESH))
        return found

    def own_copy(layer, kv):
        src = k_ref if kv == 0 else v_ref
        return pltpu.make_async_copy(src.at[layer, me], stage.at[layer, kv, me], own_sem.at[layer, kv])

    for layer in range(n_layers):
        for kv in range(2):
            for copy in sends(layer, kv):
                copy.start()
            own_copy(layer, kv).start()
    for copy in weight_copies(1):
        copy.start()

    def arrived(layer, kv):
        own_copy(layer, kv).wait()
        for copy in sends(layer, kv):
            copy.wait_recv()

    my_len = len_ref[me]
    last_slot = my_len - WINDOW
    angle_row = my_len.astype(F32) * freq_row_ref[...]
    cos_row = jnp.cos(angle_row)
    sin_row = jnp.sin(angle_row)
    angle_col = my_len.astype(F32) * freq_col_ref[...]
    cos_col = jnp.cos(angle_col)
    sin_col = jnp.sin(angle_col)
    lane_q = lax.broadcasted_iota(jnp.int32, (SUBLANES, q_width), 1)
    row_q = lax.broadcasted_iota(jnp.int32, (SUBLANES, q_width), 0)
    first_half = lax.rem(lane_q, head_dim) < half
    own_head = lax.div(lane_q, head_dim) == row_q

    residual = jnp.concatenate([hid_ref[0:1, b * LANES:(b + 1) * LANES] for b in range(blocks)], axis=0)
    out_copies = []

    def attention_query(layer, sliding):
        q = query[...]
        if sliding:
            partner = jnp.where(first_half, pltpu.roll(q, q_width - half, 1), pltpu.roll(q, half, 1))
            q = q * cos_row + jnp.where(first_half, -partner, partner) * sin_row
        q = jnp.where(own_head, q, 0.0)
        q = functools.reduce(lambda a, b: a + b, [q[:, b * LANES:(b + 1) * LANES] for b in range(q_width // LANES)])
        return (q[:, :head_dim] + q[:, head_dim:2 * head_dim]).astype(BF16)

    for layer in range(n_layers):
        sliding = layer < n_layers - 1
        slot = layer % 2
        res32 = residual.astype(F32)
        mean = jnp.sum(jnp.sum(res32, axis=1, keepdims=True), axis=0, keepdims=True) / dim
        centered = res32 - mean
        variance = jnp.sum(jnp.sum(centered * centered, axis=1, keepdims=True), axis=0, keepdims=True) / dim
        scaled = centered * lax.rsqrt(variance + NORM_EPS)
        for b in range(blocks):
            cols = slice(b * LANES, (b + 1) * LANES)
            line = scaled[b:b + 1, :] * gain_ref[layer:layer + 1, cols].astype(F32)
            normed[:, cols] = jnp.broadcast_to(line, (SUBLANES, LANES)).astype(BF16)
        waits = weight_copies(layer)
        waits[0].wait()

        @pl.loop(0, q_width // TILE)
        def _(n):
            cols = pl.ds(pl.multiple_of(n * TILE, TILE), TILE)
            query[:, cols] = jnp.dot(normed[...], wq[slot, :, cols], preferred_element_type=F32)

        q_heads = attention_query(layer, sliding)
        waits[1].wait()
        k_col = contract_lanes(wk[slot], normed[...])
        if sliding:
            first, second = k_col[:half], k_col[half:]
            k_col = jnp.concatenate([first * cos_col[:half] - second * sin_col[:half], second * cos_col[half:] + first * sin_col[half:]], axis=0)
        waits[2].wait()
        v_col = contract_lanes(wv[slot], normed[...])
        columns = (k_col[:, 0:1].astype(BF16), v_col[:, 0:1].astype(BF16))
        waits[3].wait()
        waits[4].wait()

        def gate_up(cols):
            gate = jnp.dot(normed[...], wg[slot, :, cols], preferred_element_type=F32)
            up = jnp.dot(normed[...], wu[slot, :, cols], preferred_element_type=F32)
            act[:, cols] = (gate * (1.0 / (1.0 + jnp.exp(-gate))) * up).astype(BF16)

        @pl.loop(0, ffn // TILE)
        def _(n):
            gate_up(pl.ds(pl.multiple_of(n * TILE, TILE), TILE))

        if ffn % TILE:
            gate_up(slice(ffn // TILE * TILE, ffn))
        waits[5].wait()

        @pl.loop(0, dim // TILE)
        def _(n):
            cols = pl.ds(pl.multiple_of(n * TILE, TILE), TILE)
            total[:, cols] = row_of(jnp.dot(act[...], wd[slot, :, cols], preferred_element_type=F32), 0)

        def build(kv):
            arrived(layer, kv)
            new = jnp.broadcast_to(columns[kv], (head_dim, piece))
            parts = n_low if sliding else n_sp
            for part in range(parts):
                at = slice(part * piece, (part + 1) * piece)
                ids = part * piece + lax.broadcasted_iota(jnp.int32, (head_dim, piece), 1)
                if sliding:
                    value = jnp.where(ids < last_slot, stage[layer, kv, part + n_low], stage[layer, kv, part])
                    value = jnp.where(ids == last_slot, new, value)
                    win[slot, kv, :, at] = value
                else:
                    value = jnp.where(ids < my_len, stage[layer, kv, part], jnp.zeros_like(new))
                    value = jnp.where(ids == my_len, new, value)
                    glob[kv, :, at] = value
            if sliding:
                target = win_k_out if kv == 0 else win_v_out
                copy = pltpu.make_async_copy(win.at[slot, kv], target.at[layer], out_sem.at[layer, kv])
            else:
                target = glob_k_out if kv == 0 else glob_v_out
                copy = pltpu.make_async_copy(glob.at[kv], target, out_sem.at[layer, kv])
            copy.start()
            out_copies.append(copy)

        if layer >= 2 and sliding:
            for copy in out_copies[2 * (layer - 2):2 * (layer - 1)]:
                copy.wait()
        build(0)
        keys = win[slot, 0] if sliding else glob[0]
        scores = jnp.dot(q_heads, keys, preferred_element_type=F32) * head_dim ** -0.5
        if not sliding:
            ids = lax.broadcasted_iota(jnp.int32, scores.shape, 1)
            scores = jnp.where(ids <= my_len, scores, -1e30)
        top = jnp.max(scores, axis=1, keepdims=True)
        weights = jnp.exp(scores - top)
        weights = (weights * (1.0 / jnp.sum(weights, axis=1, keepdims=True))).astype(BF16)
        build(1)
        values = win[slot, 1] if sliding else glob[1]
        mixed = contract_lanes(weights, values)
        mixed = jnp.concatenate([mixed] * n_heads, axis=1)
        mixed = jnp.where(own_head, mixed, 0.0).astype(BF16)
        waits[6].wait()

        @pl.loop(0, dim // TILE)
        def _(n):
            cols = pl.ds(pl.multiple_of(n * TILE, TILE), TILE)
            total[:, cols] += jnp.dot(mixed, wo[slot, :, cols], preferred_element_type=F32)

        if layer + 2 < n_layers:
            for copy in weight_copies(layer + 2):
                copy.start()
        for b in range(blocks):
            sums[layer, my_tp, b:b + 1, :] = jnp.sum(total[:, b * LANES:(b + 1) * LANES], axis=0, keepdims=True)
        reduces = [pltpu.make_async_remote_copy(
            src_ref=sums.at[layer, my_tp], dst_ref=sums.at[layer, my_tp],
            send_sem=sum_send_sem.at[layer, step], recv_sem=sum_recv_sem.at[layer, step],
            device_id={"tp": lax.rem(my_tp + step, n_tp)}, device_id_type=MESH) for step in range(1, n_tp)]
        for copy in reduces:
            copy.start()
        for copy in reduces:
            copy.wait_recv()
        summed = res32
        for other in range(n_tp):
            summed = summed + sums[layer, other]
        residual = summed.astype(BF16)
        for copy in reduces:
            copy.wait_send()

    for b in range(blocks):
        hid_out[0:1, b * LANES:(b + 1) * LANES] = residual[b:b + 1, :]
    waited = 2 * max(0, n_layers - 1 - 2)
    for copy in out_copies[waited:]:
        copy.wait()
    for layer in range(n_layers):
        for kv in range(2):
            for copy in sends(layer, kv):
                copy.wait_send()


def solution(mesh):
    cache_spec = P(None, "dp", "tp", "sp", None)
    row_spec = P(("dp", "sp"), None)
    col_spec = P(None, None, "tp")
    inner_spec = P(None, "tp", None)
    window_spec = P(None, ("dp", "sp"), "tp", None, None)
    global_spec = P(("dp", "sp"), "tp", None, None)
    in_specs = (cache_spec, cache_spec, P("dp"), row_spec, P(None, None), col_spec, col_spec, col_spec, inner_spec, col_spec, col_spec, inner_spec)
    out_specs = (row_spec, window_spec, window_spec, global_spec, global_spec)
    n_sp, n_tp = mesh.shape["sp"], mesh.shape["tp"]

    def device_step(k_cache, v_cache, lengths, hidden, ln_gain, w_query, w_key, w_value, w_out, w_gate, w_up, w_down):
        n_layers, dim, q_width = w_query.shape
        n_rows, _, piece, head_dim = k_cache.shape[1:]
        ffn = w_gate.shape[-1]
        seq_len = piece * n_sp
        cache_k = jnp.swapaxes(k_cache, 3, 4).reshape(n_layers, n_rows, head_dim, piece)
        cache_v = jnp.swapaxes(v_cache, 3, 4).reshape(n_layers, n_rows, head_dim, piece)
        half = head_dim // 2
        freq = np.float32(1.0) / np.power(np.float32(ROPE_BASE), np.arange(half, dtype=np.float32) * np.float32(2.0) / np.float32(head_dim))
        freq_row = np.tile(freq.astype(np.float32), (SUBLANES, q_width // half))
        freq_col = np.tile(freq.astype(np.float32)[:, None], (2, SUBLANES))
        vmem = pl.BlockSpec(memory_space=pltpu.VMEM)
        hbm = pl.BlockSpec(memory_space=pl.ANY)
        hid, win_k, win_v, glob_k, glob_v = pl.pallas_call(
            functools.partial(decode_kernel, n_sp, n_tp),
            out_shape=(
                jax.ShapeDtypeStruct((1, dim), BF16),
                jax.ShapeDtypeStruct((n_layers - 1, head_dim, WINDOW), BF16),
                jax.ShapeDtypeStruct((n_layers - 1, head_dim, WINDOW), BF16),
                jax.ShapeDtypeStruct((head_dim, seq_len), BF16),
                jax.ShapeDtypeStruct((head_dim, seq_len), BF16),
            ),
            in_specs=[pl.BlockSpec(memory_space=pltpu.SMEM)] + [vmem] * 4 + [hbm] * 9,
            out_specs=(vmem, hbm, hbm, hbm, hbm),
            scratch_shapes=[
                pltpu.VMEM((n_layers, 2, n_sp, head_dim, piece), BF16),
                pltpu.VMEM((2, dim, q_width), BF16),
                pltpu.VMEM((2, head_dim, dim), BF16),
                pltpu.VMEM((2, head_dim, dim), BF16),
                pltpu.VMEM((2, q_width, dim), BF16),
                pltpu.VMEM((2, dim, ffn), BF16),
                pltpu.VMEM((2, dim, ffn), BF16),
                pltpu.VMEM((2, ffn, dim), BF16),
                pltpu.VMEM((2, 2, head_dim, WINDOW), BF16),
                pltpu.VMEM((2, head_dim, seq_len), BF16),
                pltpu.VMEM((SUBLANES, dim), BF16),
                pltpu.VMEM((SUBLANES, q_width), F32),
                pltpu.VMEM((SUBLANES, ffn), BF16),
                pltpu.VMEM((SUBLANES, dim), F32),
                pltpu.VMEM((n_layers, n_tp, dim // LANES, LANES), F32),
                pltpu.SemaphoreType.DMA((n_layers, 2, n_sp)),
                pltpu.SemaphoreType.DMA((n_layers, 2, n_sp)),
                pltpu.SemaphoreType.DMA((n_layers, 2)),
                pltpu.SemaphoreType.DMA((2, 7)),
                pltpu.SemaphoreType.DMA((n_layers, 2)),
                pltpu.SemaphoreType.DMA((n_layers, n_tp)),
                pltpu.SemaphoreType.DMA((n_layers, n_tp)),
            ],
            compiler_params=pltpu.CompilerParams(collective_id=0, has_side_effects=True, vmem_limit_bytes=60 << 20),
        )(lengths, hidden, ln_gain, freq_row, freq_col, cache_k, cache_v, w_query, jnp.swapaxes(w_key, 1, 2), jnp.swapaxes(w_value, 1, 2), w_out, w_gate, w_up, w_down)

        def back(array):
            lead = array.shape[:-2]
            return jnp.swapaxes(array.reshape(lead + (1, 1) + array.shape[-2:]), -2, -1)

        return hid, back(win_k), back(win_v), back(glob_k), back(glob_v)

    return jax.shard_map(device_step, mesh=mesh, in_specs=in_specs, out_specs=out_specs, check_vma=False)
```

time: 472 us -> 115 us (0.24)
  the two profiles are of different devices: /device:TPU:96 before, /device:TPU:97 now
where the time goes in v1:
time: 115 us
  Pallas kernels  107 us (93%)
  local copies, waits for them, and re-layouts  7.34 us (6%)
    pallas_call x1, Pallas kernels, device_step(): pl.pallas_call(functools.partial(decode_kernel, n_sp, n_tp), out_shape=(j...  107 us
    unnamed x11, local copies, waits for them, and re-layouts  7.34 us

profile of v1, /device:TPU:97, one launch (start us, length us, event | category | flops | bytes accessed | tf_op | source)
XLA Modules:
  0.0 115.2 jit_solution(4094646048611864226)
XLA Ops:
  0.6 107.2 %shard_map.173 = (bf16[1,2048]{1,0:T(2,128)(2,1)}, bf16[3,64,4096]{2,1,0:T(8,128)(2,1)}, bf16[3,64,4096]{2,1,0:T(8,128)(2,1)}, bf16[64,8192]{1,0:T(8,128)(2,1)}, bf16[64,8192]{1,0:T(8,128)(2,1)}) custom-call(s32[8]{0:T(128)} %len_ref.1, bf16[1,2048]{1,0:T(2,128)(2,1)} %hid_ref.1, bf16[4,2048]{1,0:T(4,128)(2,1)} %gain_ref.1, ...), custom_call_target="tpu_custom_call" | custom-call | tf_op jit(solution)/shard_map/pallas_call | solution.py:270
  107.9 0.0 copy-start
  107.9 0.0 copy-start.2
  107.9 1.5 %copy.28 = bf16[1,2048]{1,0:T(2,128)(2,1)} copy(bf16[1,2048]{1,0:T(2,128)(2,1)} %get-tuple-element.25) | data formatting | bytes 8192
  109.3 0.0 copy-start.1
  109.3 2.8 %copy.29 = bf16[3,1,1,4096,64]{3,4,2,1,0:T(8,128)(2,1)} copy(bf16[3,1,1,4096,64]{3,4,2,1,0:T(8,128)(2,1)} %bitcast.31) | data formatting | bytes 3145728
  112.1 0.0 copy-done
  112.1 1.1 copy.30
  113.3 0.0 copy-done.2
  113.3 1.0 copy.31
  114.2 0.0 copy-done.1
  114.2 1.0 copy.32
Async XLA Ops:
  107.9 4.3 %copy-start = (bf16[3,64,4096]{2,1,0:T(8,128)(2,1)S(1)}, bf16[3,64,4096]{2,1,0:T(8,128)(2,1)}, u32[]{:S(2)}) copy-start(bf16[3,64,4096]{2,1,0:T(8,128)(2,1)} %get-tuple-element.12) | copy-start | bytes 4718596
  107.9 5.4 %copy-start.2 = (bf16[64,8192]{1,0:T(8,128)(2,1)S(1)}, bf16[64,8192]{1,0:T(8,128)(2,1)}, u32[]{:S(2)}) copy-start(bf16[64,8192]{1,0:T(8,128)(2,1)} %get-tuple-element.13) | copy-start | bytes 3145732
  109.3 4.9 %copy-start.1 = (bf16[64,8192]{1,0:T(8,128)(2,1)S(1)}, bf16[64,8192]{1,0:T(8,128)(2,1)}, u32[]{:S(2)}) copy-start(bf16[64,8192]{1,0:T(8,128)(2,1)} %get-tuple-element.14) | copy-start | bytes 3145732

commit v2 on v1

--- a/solution.py
+++ b/solution.py
@@ -14,6 +14,7 @@
 LANES = 128
 SUBLANES = 8
 TILE = 256
+CORES = 2
 F32 = jnp.float32
 BF16 = jnp.bfloat16
 MESH = pl.DeviceIdType.MESH
@@ -23,15 +24,20 @@
     return lax.dot_general(left, right, (((1,), (1,)), ((), ())), preferred_element_type=F32)
 
 
-def row_of(values, index):
-    rows = lax.broadcasted_iota(jnp.int32, values.shape, 0)
-    return jnp.where(rows == index, values, jnp.zeros_like(values))
+def write_kernel(*refs):
+    count = (len(refs) - 1) // 2
+    sources, targets, sem = refs[:count], refs[count:2 * count], refs[-1]
+    copies = [pltpu.make_async_copy(src, dst, sem.at[i]) for i, (src, dst) in enumerate(zip(sources, targets))]
+    for copy in copies:
+        copy.start()
+    for copy in copies:
+        copy.wait()
 
 
 def decode_kernel(n_sp, n_tp, len_ref, hid_ref, gain_ref, freq_row_ref, freq_col_ref, k_ref, v_ref, wq_ref, wk_ref, wv_ref, wo_ref, wg_ref, wu_ref, wd_ref,
                   hid_out, win_k_out, win_v_out, glob_k_out, glob_v_out,
-                  stage, wq, wk, wv, wo, wg, wu, wd, win, glob, normed, query, act, total, sums,
-                  send_sem, recv_sem, own_sem, weight_sem, out_sem, sum_send_sem, sum_recv_sem):
+                  stage, wq, wk, wv, wo, wg, wu, wd, normed, query, act, mlp, sums,
+                  send_sem, recv_sem, own_sem, weight_sem, sum_send_sem, sum_recv_sem):
     n_layers = wq_ref.shape[0]
     piece = k_ref.shape[-1]
     head_dim = k_ref.shape[-2]
@@ -61,16 +67,26 @@
         pl.semaphore_signal(barrier, inc=1, device_id={"tp": lax.rem(my_tp + step, n_tp)}, device_id_type=MESH)
     pl.semaphore_wait(barrier, n_sp + n_tp - 2)
 
+    chips = n_sp // CORES
+    chip, core = lax.div(me, CORES), lax.rem(me, CORES)
+    far_first = sorted(range(1, chips), key=lambda d: -min(d, chips - d))
+    chip_order = [0] + far_first
+    deltas = [(dc, dk) for dc in chip_order for dk in range(CORES) if (dc, dk) != (0, 0)]
+
+    def shifted(dc, dk):
+        return lax.rem(chip + dc, chips) * CORES + lax.rem(core + dk, CORES)
+
+    def send(layer, kv, dc, dk):
+        src = k_ref if kv == 0 else v_ref
+        dst = shifted(dc, dk)
+        at = dc * CORES + dk
+        return pltpu.make_async_remote_copy(
+            src_ref=src.at[layer, dst], dst_ref=stage.at[layer, kv, me],
+            send_sem=send_sem.at[layer, kv, at], recv_sem=recv_sem.at[layer, kv, at],
+            device_id={"sp": dst}, device_id_type=MESH)
+
     def sends(layer, kv):
-        src = k_ref if kv == 0 else v_ref
-        found = []
-        for step in range(1, n_sp):
-            dst = lax.rem(me + step, n_sp)
-            found.append(pltpu.make_async_remote_copy(
-                src_ref=src.at[layer, dst], dst_ref=stage.at[layer, kv, me],
-                send_sem=send_sem.at[layer, kv, step], recv_sem=recv_sem.at[layer, kv, step],
-                device_id={"sp": dst}, device_id_type=MESH))
-        return found
+        return [send(layer, kv, dc, dk) for dc, dk in deltas]
 
     def own_copy(layer, kv):
         src = k_ref if kv == 0 else v_ref
@@ -84,10 +100,11 @@
     for copy in weight_copies(1):
         copy.start()
 
-    def arrived(layer, kv):
-        own_copy(layer, kv).wait()
-        for copy in sends(layer, kv):
-            copy.wait_recv()
+    def wait_from(layer, kv, dc, dk):
+        if (dc, dk) == (0, 0):
+            own_copy(layer, kv).wait()
+        else:
+            send(layer, kv, (chips - dc) % chips, dk).wait_recv()
 
     my_len = len_ref[me]
     last_slot = my_len - WINDOW
@@ -103,7 +120,6 @@
     own_head = lax.div(lane_q, head_dim) == row_q
 
     residual = jnp.concatenate([hid_ref[0:1, b * LANES:(b + 1) * LANES] for b in range(blocks)], axis=0)
-    out_copies = []
 
     def attention_query(layer, sliding):
         q = query[...]
@@ -162,61 +178,60 @@
         @pl.loop(0, dim // TILE)
         def _(n):
             cols = pl.ds(pl.multiple_of(n * TILE, TILE), TILE)
-            total[:, cols] = row_of(jnp.dot(act[...], wd[slot, :, cols], preferred_element_type=F32), 0)
-
-        def build(kv):
-            arrived(layer, kv)
+            down = jnp.dot(act[...], wd[slot, :, cols], preferred_element_type=F32)
+            mlp[:, cols] = down[0:1]
+
+        def pieces(kv):
             new = jnp.broadcast_to(columns[kv], (head_dim, piece))
-            parts = n_low if sliding else n_sp
-            for part in range(parts):
-                at = slice(part * piece, (part + 1) * piece)
-                ids = part * piece + lax.broadcasted_iota(jnp.int32, (head_dim, piece), 1)
-                if sliding:
-                    value = jnp.where(ids < last_slot, stage[layer, kv, part + n_low], stage[layer, kv, part])
-                    value = jnp.where(ids == last_slot, new, value)
-                    win[slot, kv, :, at] = value
-                else:
-                    value = jnp.where(ids < my_len, stage[layer, kv, part], jnp.zeros_like(new))
-                    value = jnp.where(ids == my_len, new, value)
-                    glob[kv, :, at] = value
+            lanes = lax.broadcasted_iota(jnp.int32, (head_dim, piece), 1)
             if sliding:
-                target = win_k_out if kv == 0 else win_v_out
-                copy = pltpu.make_async_copy(win.at[slot, kv], target.at[layer], out_sem.at[layer, kv])
+                target = (win_k_out if kv == 0 else win_v_out).at[layer]
+                half_chips = chips // 2
+                for dc in sorted(range(half_chips)):
+                    for dk in range(CORES):
+                        wait_from(layer, kv, dc, dk)
+                        wait_from(layer, kv, dc + half_chips, dk)
+                        part = lax.rem(shifted(dc, dk), n_low)
+                        ids = part * piece + lanes
+                        value = jnp.where(ids < last_slot, stage[layer, kv, part + n_low], stage[layer, kv, part])
+                        value = jnp.where(ids == last_slot, new, value)
+                        target[:, pl.ds(pl.multiple_of(part * piece, piece), piece)] = value
+                        yield part, value
             else:
                 target = glob_k_out if kv == 0 else glob_v_out
-                copy = pltpu.make_async_copy(glob.at[kv], target, out_sem.at[layer, kv])
-            copy.start()
-            out_copies.append(copy)
-
-        if layer >= 2 and sliding:
-            for copy in out_copies[2 * (layer - 2):2 * (layer - 1)]:
-                copy.wait()
-        build(0)
-        keys = win[slot, 0] if sliding else glob[0]
-        scores = jnp.dot(q_heads, keys, preferred_element_type=F32) * head_dim ** -0.5
-        if not sliding:
-            ids = lax.broadcasted_iota(jnp.int32, scores.shape, 1)
-            scores = jnp.where(ids <= my_len, scores, -1e30)
-        top = jnp.max(scores, axis=1, keepdims=True)
-        weights = jnp.exp(scores - top)
-        weights = (weights * (1.0 / jnp.sum(weights, axis=1, keepdims=True))).astype(BF16)
-        build(1)
-        values = win[slot, 1] if sliding else glob[1]
-        mixed = contract_lanes(weights, values)
-        mixed = jnp.concatenate([mixed] * n_heads, axis=1)
-        mixed = jnp.where(own_head, mixed, 0.0).astype(BF16)
+                for dc in chip_order:
+                    for dk in range(CORES):
+                        wait_from(layer, kv, dc, dk)
+                        part = shifted(dc, dk)
+                        ids = part * piece + lanes
+                        value = jnp.where(ids < my_len, stage[layer, kv, part], jnp.zeros_like(new))
+                        value = jnp.where(ids == my_len, new, value)
+                        target[:, pl.ds(pl.multiple_of(part * piece, piece), piece)] = value
+                        yield part, value
+
+        scores = []
+        for part, keys in pieces(0):
+            score = jnp.dot(q_heads, keys, preferred_element_type=F32) * head_dim ** -0.5
+            if not sliding:
+                ids = part * piece + lax.broadcasted_iota(jnp.int32, score.shape, 1)
+                score = jnp.where(ids <= my_len, score, -1e30)
+            scores.append(score)
+        top = functools.reduce(jnp.maximum, [jnp.max(score, axis=1, keepdims=True) for score in scores])
+        scores = [jnp.exp(score - top) for score in scores]
+        share = 1.0 / functools.reduce(jnp.add, [jnp.sum(score, axis=1, keepdims=True) for score in scores])
+        weights = [(score * share).astype(BF16) for score in scores]
+        mixed = functools.reduce(jnp.add, [contract_lanes(weight, values) for weight, (part, values) in zip(weights, pieces(1))])
+        mixed = jnp.where(own_head, jnp.concatenate([mixed] * n_heads, axis=1), 0.0)
+        mixed = jnp.broadcast_to(jnp.sum(mixed, axis=0, keepdims=True), mixed.shape).astype(BF16)
         waits[6].wait()
-
-        @pl.loop(0, dim // TILE)
-        def _(n):
-            cols = pl.ds(pl.multiple_of(n * TILE, TILE), TILE)
-            total[:, cols] += jnp.dot(mixed, wo[slot, :, cols], preferred_element_type=F32)
-
+        for n in range(dim // TILE):
+            attn = jnp.dot(mixed, wo[slot, :, n * TILE:(n + 1) * TILE], preferred_element_type=F32)
+            for b in range(n * TILE // LANES, (n + 1) * TILE // LANES):
+                inner = slice(b * LANES - n * TILE, (b + 1) * LANES - n * TILE)
+                sums[layer, my_tp, b:b + 1, :] = attn[0:1, inner] + mlp[:, b * LANES:(b + 1) * LANES]
         if layer + 2 < n_layers:
             for copy in weight_copies(layer + 2):
                 copy.start()
-        for b in range(blocks):
-            sums[layer, my_tp, b:b + 1, :] = jnp.sum(total[:, b * LANES:(b + 1) * LANES], axis=0, keepdims=True)
         reduces = [pltpu.make_async_remote_copy(
             src_ref=sums.at[layer, my_tp], dst_ref=sums.at[layer, my_tp],
             send_sem=sum_send_sem.at[layer, step], recv_sem=sum_recv_sem.at[layer, step],
@@ -234,9 +249,6 @@
 
     for b in range(blocks):
         hid_out[0:1, b * LANES:(b + 1) * LANES] = residual[b:b + 1, :]
-    waited = 2 * max(0, n_layers - 1 - 2)
-    for copy in out_copies[waited:]:
-        copy.wait()
     for layer in range(n_layers):
         for kv in range(2):
             for copy in sends(layer, kv):
@@ -267,17 +279,12 @@
         freq_col = np.tile(freq.astype(np.float32)[:, None], (2, SUBLANES))
         vmem = pl.BlockSpec(memory_space=pltpu.VMEM)
         hbm = pl.BlockSpec(memory_space=pl.ANY)
-        hid, win_k, win_v, glob_k, glob_v = pl.pallas_call(
+        shapes = [(1, dim)] + [(n_layers - 1, head_dim, WINDOW)] * 2 + [(head_dim, seq_len)] * 2
+        results = pl.pallas_call(
             functools.partial(decode_kernel, n_sp, n_tp),
-            out_shape=(
-                jax.ShapeDtypeStruct((1, dim), BF16),
-                jax.ShapeDtypeStruct((n_layers - 1, head_dim, WINDOW), BF16),
-                jax.ShapeDtypeStruct((n_layers - 1, head_dim, WINDOW), BF16),
-                jax.ShapeDtypeStruct((head_dim, seq_len), BF16),
-                jax.ShapeDtypeStruct((head_dim, seq_len), BF16),
-            ),
+            out_shape=[pltpu.VMEM(shape, BF16) for shape in shapes],
             in_specs=[pl.BlockSpec(memory_space=pltpu.SMEM)] + [vmem] * 4 + [hbm] * 9,
-            out_specs=(vmem, hbm, hbm, hbm, hbm),
+            out_specs=[vmem] * len(shapes),
             scratch_shapes=[
                 pltpu.VMEM((n_layers, 2, n_sp, head_dim, piece), BF16),
                 pltpu.VMEM((2, dim, q_width), BF16),
@@ -287,23 +294,29 @@
                 pltpu.VMEM((2, dim, ffn), BF16),
                 pltpu.VMEM((2, dim, ffn), BF16),
                 pltpu.VMEM((2, ffn, dim), BF16),
-                pltpu.VMEM((2, 2, head_dim, WINDOW), BF16),
-                pltpu.VMEM((2, head_dim, seq_len), BF16),
                 pltpu.VMEM((SUBLANES, dim), BF16),
                 pltpu.VMEM((SUBLANES, q_width), F32),
                 pltpu.VMEM((SUBLANES, ffn), BF16),
-                pltpu.VMEM((SUBLANES, dim), F32),
+                pltpu.VMEM((1, dim), F32),
                 pltpu.VMEM((n_layers, n_tp, dim // LANES, LANES), F32),
                 pltpu.SemaphoreType.DMA((n_layers, 2, n_sp)),
                 pltpu.SemaphoreType.DMA((n_layers, 2, n_sp)),
                 pltpu.SemaphoreType.DMA((n_layers, 2)),
                 pltpu.SemaphoreType.DMA((2, 7)),
-                pltpu.SemaphoreType.DMA((n_layers, 2)),
                 pltpu.SemaphoreType.DMA((n_layers, n_tp)),
                 pltpu.SemaphoreType.DMA((n_layers, n_tp)),
             ],
-            compiler_params=pltpu.CompilerParams(collective_id=0, has_side_effects=True, vmem_limit_bytes=60 << 20),
+            compiler_params=pltpu.CompilerParams(collective_id=0, has_side_effects=True, vmem_limit_bytes=53 << 20),
         )(lengths, hidden, ln_gain, freq_row, freq_col, cache_k, cache_v, w_query, jnp.swapaxes(w_key, 1, 2), jnp.swapaxes(w_value, 1, 2), w_out, w_gate, w_up, w_down)
+
+        hid, win_k, win_v, glob_k, glob_v = pl.pallas_call(
+            write_kernel,
+            out_shape=[jax.ShapeDtypeStruct(shape, BF16) for shape in shapes],
+            in_specs=[vmem] * len(shapes),
+            out_specs=[hbm] * len(shapes),
+            scratch_shapes=[pltpu.SemaphoreType.DMA((len(shapes),))],
+            compiler_params=pltpu.CompilerParams(vmem_limit_bytes=1 << 20),
+        )(*[pltpu.with_memory_space_constraint(result, pltpu.VMEM) for result in results])
 
         def back(array):
             lead = array.shape[:-2]

time: 115 us -> 108 us (0.939)
  local copies, waits for them, and re-layouts: 7.34 us -> 0 us
    unnamed x11 -> x0, local copies, waits for them, and re-layouts: 7.34 us -> none
    pallas_call x1 -> x2, Pallas kernels: 107 us -> 108 us  [the longest x1 105 us: device_step(): pl.pallas_call(functools.partial(decode_kernel, n_sp, n_tp), out_shape=[p...]
where the time goes in v2:
time: 108 us
  Pallas kernels  108 us (100%)
    pallas_call x1, Pallas kernels, device_step(): pl.pallas_call(functools.partial(decode_kernel, n_sp, n_tp), out_shape=[p...  105 us
    pallas_call x1, Pallas kernels, device_step(): pl.pallas_call(write_kernel, out_shape=[jax.ShapeDtypeStruct(shape, BF16)...  2.4 us

profile of v2, /device:TPU:97, one launch (start us, length us, event | category | flops | bytes accessed | tf_op | source)
XLA Modules:
  0.0 108.3 jit_solution(17717519221519397757)
XLA Ops:
  0.6 105.3 %shard_map.173 = (bf16[1,2048]{1,0:T(2,128)(2,1)S(1)}, bf16[3,64,4096]{2,1,0:T(8,128)(2,1)S(1)}, bf16[3,64,4096]{2,1,0:T(8,128)(2,1)S(1)}, bf16[64,8192]{1,0:T(8,128)(2,1)S(1)}, bf16[64,8192]{1,0:T(8,128)(2,1)S(1)}) custom-call(s32[8]{0:T(128)} %len_ref.1, bf16[1,2048]{1,0:T(2,128)(2,1)} %hid_ref.1, bf16[4,2048]{1,0:T(4,128)(2,1)} %gain_ref.1, ...), custom_call_target="tpu_custom_call" | custom-call | tf_op jit(solution)/shard_map/pallas_call | solution.py:283
  105.9 2.4 %shard_map.174 = (bf16[1,2048]{1,0:T(2,128)(2,1)}, bf16[3,64,4096]{2,1,0:T(8,128)(2,1)}, bf16[3,64,4096]{2,1,0:T(8,128)(2,1)}, bf16[64,8192]{1,0:T(8,128)(2,1)}, bf16[64,8192]{1,0:T(8,128)(2,1)}) custom-call(bf16[1,2048]{1,0:T(2,128)(2,1)S(1)} %get-tuple-element.15.refs_0_, bf16[3,64,4096]{2,1,0:T(8,128)(2,1)S(1)} %get-tuple-element.16.refs_1_, ...), custom_call_target="tpu_custom_call" | custom-call | tf_op jit(solution)/shard_map/pallas_call | solution.py:312

commit v3 on v2

--- a/solution.py
+++ b/solution.py
@@ -34,10 +34,11 @@
         copy.wait()
 
 
-def decode_kernel(n_sp, n_tp, len_ref, hid_ref, gain_ref, freq_row_ref, freq_col_ref, k_ref, v_ref, wq_ref, wk_ref, wv_ref, wo_ref, wg_ref, wu_ref, wd_ref,
+def decode_kernel(n_sp, n_tp, len_in, hid_in, gain_in, freq_row_in, freq_col_in, k_ref, v_ref, wq_ref, wk_ref, wv_ref, wo_ref, wg_ref, wu_ref, wd_ref,
                   hid_out, win_k_out, win_v_out, glob_k_out, glob_v_out,
-                  stage, wq, wk, wv, wo, wg, wu, wd, normed, query, act, mlp, sums,
-                  send_sem, recv_sem, own_sem, weight_sem, sum_send_sem, sum_recv_sem):
+                  stage, wq, wk, wv, wo, wg, wu, wd, normed, query, act, mlp, sums, len_ref, hid_ref, gain_ref, freq_row_ref, freq_col_ref,
+                  local, local_score, queries, stats, values_out, values_in,
+                  send_sem, recv_sem, own_sem, weight_sem, small_sem, sum_send_sem, sum_recv_sem, local_sem, message_send_sem, message_recv_sem, line_sem, ready_sem):
     n_layers = wq_ref.shape[0]
     piece = k_ref.shape[-1]
     head_dim = k_ref.shape[-2]
@@ -57,15 +58,20 @@
         slot = layer % 2
         return [pltpu.make_async_copy(src.at[layer], dst.at[slot], weight_sem.at[slot, i]) for i, (src, dst) in enumerate(weight_pairs)]
 
-    for copy in weight_copies(0):
-        copy.start()
-
     barrier = pltpu.get_barrier_semaphore()
     for step in range(1, n_sp):
         pl.semaphore_signal(barrier, inc=1, device_id={"sp": lax.rem(me + step, n_sp)}, device_id_type=MESH)
-    for step in range(1, n_tp):
-        pl.semaphore_signal(barrier, inc=1, device_id={"tp": lax.rem(my_tp + step, n_tp)}, device_id_type=MESH)
-    pl.semaphore_wait(barrier, n_sp + n_tp - 2)
+    lead = me == 0
+
+    @pl.when(lead)
+    def _():
+        for step in range(1, n_tp):
+            pl.semaphore_signal(barrier, inc=1, device_id={"tp": lax.rem(my_tp + step, n_tp)}, device_id_type=MESH)
+        pl.semaphore_wait(barrier, n_sp + n_tp - 2)
+
+    @pl.when(jnp.logical_not(lead))
+    def _():
+        pl.semaphore_wait(barrier, n_sp - 1)
 
     chips = n_sp // CORES
     chip, core = lax.div(me, CORES), lax.rem(me, CORES)
@@ -92,13 +98,42 @@
         src = k_ref if kv == 0 else v_ref
         return pltpu.make_async_copy(src.at[layer, me], stage.at[layer, kv, me], own_sem.at[layer, kv])
 
-    for layer in range(n_layers):
-        for kv in range(2):
-            for copy in sends(layer, kv):
-                copy.start()
-            own_copy(layer, kv).start()
-    for copy in weight_copies(1):
+    def start_bulk(layer, kv):
+        for copy in sends(layer, kv):
+            copy.start()
+        own_copy(layer, kv).start()
+
+    bulk_order = [(layer, kv) for layer in list(range(1, n_layers)) + [0] for kv in range(2)]
+    start_bulk(*bulk_order[0])
+    small_pairs = ((len_in, len_ref), (hid_in, hid_ref), (gain_in, gain_ref), (freq_row_in, freq_row_ref), (freq_col_in, freq_col_ref))
+    small_copies = [pltpu.make_async_copy(src, dst, small_sem.at[i]) for i, (src, dst) in enumerate(small_pairs)]
+    local_copies = [pltpu.make_async_copy(src.at[0], local.at[kv], local_sem.at[kv]) for kv, src in enumerate((k_ref, v_ref))]
+    first_weights = weight_copies(0)
+    for copy in small_copies + first_weights[:3]:
         copy.start()
+
+    @pl.when(lead)
+    def _():
+        for step in range(1, n_tp):
+            pl.semaphore_signal(line_sem, inc=1, device_id={"tp": lax.rem(my_tp + step, n_tp)}, device_id_type=MESH)
+        pl.semaphore_wait(line_sem, n_tp - 1)
+        for step in range(1, n_sp):
+            pl.semaphore_signal(ready_sem, inc=1, device_id={"sp": lax.rem(me + step, n_sp)}, device_id_type=MESH)
+
+    for copy in small_copies:
+        copy.wait()
+
+    def messages(kind, source, target):
+        found = []
+        for step in range(1, n_sp):
+            dst = lax.rem(me + step, n_sp)
+            found.append(pltpu.make_async_remote_copy(
+                src_ref=source(dst), dst_ref=target,
+                send_sem=message_send_sem.at[kind, step], recv_sem=message_recv_sem.at[kind, step],
+                device_id={"sp": dst}, device_id_type=MESH))
+        for copy in found:
+            copy.start()
+        return found
 
     def wait_from(layer, kv, dc, dk):
         if (dc, dk) == (0, 0):
@@ -121,6 +156,9 @@
 
     residual = jnp.concatenate([hid_ref[0:1, b * LANES:(b + 1) * LANES] for b in range(blocks)], axis=0)
 
+    lane_t = lax.broadcasted_iota(jnp.int32, (SUBLANES, LANES), 1)
+    all_messages = []
+
     def attention_query(layer, sliding):
         q = query[...]
         if sliding:
@@ -128,7 +166,87 @@
             q = q * cos_row + jnp.where(first_half, -partner, partner) * sin_row
         q = jnp.where(own_head, q, 0.0)
         q = functools.reduce(lambda a, b: a + b, [q[:, b * LANES:(b + 1) * LANES] for b in range(q_width // LANES)])
-        return (q[:, :head_dim] + q[:, head_dim:2 * head_dim]).astype(BF16)
+        return (q + pltpu.roll(q, head_dim, 1)).astype(BF16)
+
+    def pieces(layer, kv, columns):
+        sliding = layer < n_layers - 1
+        new = jnp.broadcast_to(columns[kv], (head_dim, piece))
+        lanes = lax.broadcasted_iota(jnp.int32, (head_dim, piece), 1)
+        if sliding:
+            target = (win_k_out if kv == 0 else win_v_out).at[layer]
+            half_chips = chips // 2
+            for dc in sorted(range(half_chips)):
+                for dk in range(CORES):
+                    wait_from(layer, kv, dc, dk)
+                    wait_from(layer, kv, dc + half_chips, dk)
+                    part = lax.rem(shifted(dc, dk), n_low)
+                    ids = part * piece + lanes
+                    value = jnp.where(ids < last_slot, stage[layer, kv, part + n_low], stage[layer, kv, part])
+                    value = jnp.where(ids == last_slot, new, value)
+                    target[:, pl.ds(pl.multiple_of(part * piece, piece), piece)] = value
+                    yield part, value
+        else:
+            target = glob_k_out if kv == 0 else glob_v_out
+            for dc in chip_order:
+                for dk in range(CORES):
+                    wait_from(layer, kv, dc, dk)
+                    part = shifted(dc, dk)
+                    ids = part * piece + lanes
+                    value = jnp.where(ids < my_len, stage[layer, kv, part], jnp.zeros_like(new))
+                    value = jnp.where(ids == my_len, new, value)
+                    target[:, pl.ds(pl.multiple_of(part * piece, piece), piece)] = value
+                    yield part, value
+
+    def spread_attention(q_heads, k_new, v_row, sent):
+        for copy in sent:
+            copy.wait_recv()
+        local_copies[0].wait()
+        positions = me * piece + lax.broadcasted_iota(jnp.int32, (SUBLANES, piece), 1)
+        new_score = jnp.dot(q_heads, jnp.broadcast_to(k_new, (head_dim, LANES)), preferred_element_type=F32) * head_dim ** -0.5
+        tops = jnp.zeros((SUBLANES, LANES), F32)
+        norms = jnp.zeros((SUBLANES, LANES), F32)
+        for row in range(n_sp):
+            score = jnp.dot(queries[row][:, :head_dim].astype(BF16), local[0, row], preferred_element_type=F32) * head_dim ** -0.5
+            valid = (positions > len_ref[row] - WINDOW) & (positions < len_ref[row])
+            score = jnp.where(valid, score, -1e30)
+            local_score[row] = score
+            top = jnp.max(score, axis=1, keepdims=True)
+            norm = jnp.sum(jnp.exp(score - top), axis=1, keepdims=True)
+            tops = jnp.where(lane_t == row, top, tops)
+            norms = jnp.where(lane_t == row, norm, norms)
+        mine = lane_t == me
+        raised = jnp.where(mine, jnp.maximum(tops, new_score), tops)
+        norms = jnp.where(mine, norms * jnp.exp(tops - raised) + jnp.exp(jnp.where(mine, new_score - raised, 0.0)), norms)
+        stats[me, 0] = raised
+        stats[me, 1] = norms
+        sent = messages(1, lambda dst: stats.at[me], stats.at[me])
+        all_messages.extend(sent)
+        start_bulk(*bulk_order[2])
+        for copy in weight_copies(1):
+            copy.start()
+        for copy in sent:
+            copy.wait_recv()
+        local_copies[1].wait()
+        top = functools.reduce(jnp.maximum, [stats[src, 0] for src in range(n_sp)])
+        norm = functools.reduce(jnp.add, [stats[src, 1] * jnp.exp(stats[src, 0] - top) for src in range(n_sp)])
+        share = 1.0 / jnp.where(lane_t < n_sp, norm, 1.0)
+        for row in range(n_sp):
+            weight = (jnp.exp(local_score[row] - top[:, row:row + 1]) * share[:, row:row + 1]).astype(BF16)
+            partial = contract_lanes(weight, local[1, row])
+            values_out[row] = jnp.concatenate([partial, partial], axis=1)
+        sent = messages(2, lambda dst: values_out.at[dst], values_in.at[me])
+        all_messages.extend(sent)
+        for group in bulk_order[3:]:
+            start_bulk(*group)
+        my_top = jnp.sum(jnp.where(mine, top, 0.0), axis=1, keepdims=True)
+        my_share = jnp.sum(jnp.where(mine, share, 0.0), axis=1, keepdims=True)
+        new_weight = (jnp.exp(new_score[:, 0:1] - my_top) * my_share).astype(BF16).astype(F32)
+        mixed = new_weight * v_row + values_out[me][:, :head_dim]
+        for copy in sent:
+            copy.wait_recv()
+        for step in range(1, n_sp):
+            mixed = mixed + values_in[lax.rem(me + step, n_sp)][:, :head_dim]
+        return mixed
 
     for layer in range(n_layers):
         sliding = layer < n_layers - 1
@@ -142,7 +260,7 @@
             cols = slice(b * LANES, (b + 1) * LANES)
             line = scaled[b:b + 1, :] * gain_ref[layer:layer + 1, cols].astype(F32)
             normed[:, cols] = jnp.broadcast_to(line, (SUBLANES, LANES)).astype(BF16)
-        waits = weight_copies(layer)
+        waits = first_weights if layer == 0 else weight_copies(layer)
         waits[0].wait()
 
         @pl.loop(0, q_width // TILE)
@@ -150,7 +268,15 @@
             cols = pl.ds(pl.multiple_of(n * TILE, TILE), TILE)
             query[:, cols] = jnp.dot(normed[...], wq[slot, :, cols], preferred_element_type=F32)
 
-        q_heads = attention_query(layer, sliding)
+        q_wide = attention_query(layer, sliding)
+        q_heads = q_wide[:, :head_dim]
+        if layer == 0:
+            queries[me] = q_wide.astype(F32)
+            sent = messages(0, lambda dst: queries.at[me], queries.at[me])
+            all_messages.extend(sent)
+            start_bulk(*bulk_order[1])
+            for copy in local_copies + first_weights[3:]:
+                copy.start()
         waits[1].wait()
         k_col = contract_lanes(wk[slot], normed[...])
         if sliding:
@@ -159,6 +285,10 @@
         waits[2].wait()
         v_col = contract_lanes(wv[slot], normed[...])
         columns = (k_col[:, 0:1].astype(BF16), v_col[:, 0:1].astype(BF16))
+        if layer == 0:
+            first_columns = columns
+            v_row = contract_lanes(normed[...], wv[slot]).astype(BF16).astype(F32)
+            mixed = spread_attention(q_heads, columns[0], v_row, sent)
         waits[3].wait()
         waits[4].wait()
 
@@ -181,46 +311,19 @@
             down = jnp.dot(act[...], wd[slot, :, cols], preferred_element_type=F32)
             mlp[:, cols] = down[0:1]
 
-        def pieces(kv):
-            new = jnp.broadcast_to(columns[kv], (head_dim, piece))
-            lanes = lax.broadcasted_iota(jnp.int32, (head_dim, piece), 1)
-            if sliding:
-                target = (win_k_out if kv == 0 else win_v_out).at[layer]
-                half_chips = chips // 2
-                for dc in sorted(range(half_chips)):
-                    for dk in range(CORES):
-                        wait_from(layer, kv, dc, dk)
-                        wait_from(layer, kv, dc + half_chips, dk)
-                        part = lax.rem(shifted(dc, dk), n_low)
-                        ids = part * piece + lanes
-                        value = jnp.where(ids < last_slot, stage[layer, kv, part + n_low], stage[layer, kv, part])
-                        value = jnp.where(ids == last_slot, new, value)
-                        target[:, pl.ds(pl.multiple_of(part * piece, piece), piece)] = value
-                        yield part, value
-            else:
-                target = glob_k_out if kv == 0 else glob_v_out
-                for dc in chip_order:
-                    for dk in range(CORES):
-                        wait_from(layer, kv, dc, dk)
-                        part = shifted(dc, dk)
-                        ids = part * piece + lanes
-                        value = jnp.where(ids < my_len, stage[layer, kv, part], jnp.zeros_like(new))
-                        value = jnp.where(ids == my_len, new, value)
-                        target[:, pl.ds(pl.multiple_of(part * piece, piece), piece)] = value
-                        yield part, value
-
-        scores = []
-        for part, keys in pieces(0):
-            score = jnp.dot(q_heads, keys, preferred_element_type=F32) * head_dim ** -0.5
-            if not sliding:
-                ids = part * piece + lax.broadcasted_iota(jnp.int32, score.shape, 1)
-                score = jnp.where(ids <= my_len, score, -1e30)
-            scores.append(score)
-        top = functools.reduce(jnp.maximum, [jnp.max(score, axis=1, keepdims=True) for score in scores])
-        scores = [jnp.exp(score - top) for score in scores]
-        share = 1.0 / functools.reduce(jnp.add, [jnp.sum(score, axis=1, keepdims=True) for score in scores])
-        weights = [(score * share).astype(BF16) for score in scores]
-        mixed = functools.reduce(jnp.add, [contract_lanes(weight, values) for weight, (part, values) in zip(weights, pieces(1))])
+        if layer > 0:
+            scores = []
+            for part, keys in pieces(layer, 0, columns):
+                score = jnp.dot(q_heads, keys, preferred_element_type=F32) * head_dim ** -0.5
+                if not sliding:
+                    ids = part * piece + lax.broadcasted_iota(jnp.int32, score.shape, 1)
+                    score = jnp.where(ids <= my_len, score, -1e30)
+                scores.append(score)
+            top = functools.reduce(jnp.maximum, [jnp.max(score, axis=1, keepdims=True) for score in scores])
+            scores = [jnp.exp(score - top) for score in scores]
+            share = 1.0 / functools.reduce(jnp.add, [jnp.sum(score, axis=1, keepdims=True) for score in scores])
+            weights = [(score * share).astype(BF16) for score in scores]
+            mixed = functools.reduce(jnp.add, [contract_lanes(weight, values) for weight, (part, values) in zip(weights, pieces(layer, 1, columns))])
         mixed = jnp.where(own_head, jnp.concatenate([mixed] * n_heads, axis=1), 0.0)
         mixed = jnp.broadcast_to(jnp.sum(mixed, axis=0, keepdims=True), mixed.shape).astype(BF16)
         waits[6].wait()
@@ -236,6 +339,11 @@
             src_ref=sums.at[layer, my_tp], dst_ref=sums.at[layer, my_tp],
             send_sem=sum_send_sem.at[layer, step], recv_sem=sum_recv_sem.at[layer, step],
             device_id={"tp": lax.rem(my_tp + step, n_tp)}, device_id_type=MESH) for step in range(1, n_tp)]
+        if layer == 0:
+            @pl.when(jnp.logical_not(lead))
+            def _():
+                pl.semaphore_wait(ready_sem, 1)
+
         for copy in reduces:
             copy.start()
         for copy in reduces:
@@ -249,6 +357,11 @@
 
     for b in range(blocks):
         hid_out[0:1, b * LANES:(b + 1) * LANES] = residual[b:b + 1, :]
+    for kv in range(2):
+        for _ in pieces(0, kv, first_columns):
+            pass
+    for copy in all_messages:
+        copy.wait_send()
     for layer in range(n_layers):
         for kv in range(2):
             for copy in sends(layer, kv):
@@ -283,7 +396,7 @@
         results = pl.pallas_call(
             functools.partial(decode_kernel, n_sp, n_tp),
             out_shape=[pltpu.VMEM(shape, BF16) for shape in shapes],
-            in_specs=[pl.BlockSpec(memory_space=pltpu.SMEM)] + [vmem] * 4 + [hbm] * 9,
+            in_specs=[hbm] * 14,
             out_specs=[vmem] * len(shapes),
             scratch_shapes=[
                 pltpu.VMEM((n_layers, 2, n_sp, head_dim, piece), BF16),
@@ -299,14 +412,31 @@
                 pltpu.VMEM((SUBLANES, ffn), BF16),
                 pltpu.VMEM((1, dim), F32),
                 pltpu.VMEM((n_layers, n_tp, dim // LANES, LANES), F32),
+                pltpu.SMEM(lengths.shape, jnp.int32),
+                pltpu.VMEM(hidden.shape, BF16),
+                pltpu.VMEM(ln_gain.shape, BF16),
+                pltpu.VMEM(freq_row.shape, F32),
+                pltpu.VMEM(freq_col.shape, F32),
+                pltpu.VMEM((2, n_rows, head_dim, piece), BF16),
+                pltpu.VMEM((n_rows, SUBLANES, piece), F32),
+                pltpu.VMEM((n_sp, SUBLANES, LANES), F32),
+                pltpu.VMEM((n_sp, 2, SUBLANES, LANES), F32),
+                pltpu.VMEM((n_sp, SUBLANES, LANES), F32),
+                pltpu.VMEM((n_sp, SUBLANES, LANES), F32),
                 pltpu.SemaphoreType.DMA((n_layers, 2, n_sp)),
                 pltpu.SemaphoreType.DMA((n_layers, 2, n_sp)),
                 pltpu.SemaphoreType.DMA((n_layers, 2)),
                 pltpu.SemaphoreType.DMA((2, 7)),
+                pltpu.SemaphoreType.DMA((5,)),
                 pltpu.SemaphoreType.DMA((n_layers, n_tp)),
                 pltpu.SemaphoreType.DMA((n_layers, n_tp)),
+                pltpu.SemaphoreType.DMA((2,)),
+                pltpu.SemaphoreType.DMA((3, n_sp)),
+                pltpu.SemaphoreType.DMA((3, n_sp)),
+                pltpu.SemaphoreType.REGULAR,
+                pltpu.SemaphoreType.REGULAR,
             ],
-            compiler_params=pltpu.CompilerParams(collective_id=0, has_side_effects=True, vmem_limit_bytes=53 << 20),
+            compiler_params=pltpu.CompilerParams(collective_id=0, has_side_effects=True, vmem_limit_bytes=55 << 20),
         )(lengths, hidden, ln_gain, freq_row, freq_col, cache_k, cache_v, w_query, jnp.swapaxes(w_key, 1, 2), jnp.swapaxes(w_value, 1, 2), w_out, w_gate, w_up, w_down)
 
         hid, win_k, win_v, glob_k, glob_v = pl.pallas_call(

time: 108 us -> 103 us (0.954)
  Pallas kernels: 108 us -> 102 us
    pallas_call x1, Pallas kernels: 105 us -> 99.6 us  [device_step(): pl.pallas_call(functools.partial(decode_kernel, n_sp, n_tp), out_shape=[p...]
where the time goes in v3:
time: 103 us
  Pallas kernels  102 us (99%)
    pallas_call x1, Pallas kernels, device_step(): pl.pallas_call(functools.partial(decode_kernel, n_sp, n_tp), out_shape=[p...  99.6 us
    pallas_call x1, Pallas kernels, device_step(): pl.pallas_call(write_kernel, out_shape=[jax.ShapeDtypeStruct(shape, BF16)...  2.4 us

profile of v3, /device:TPU:97, one launch (start us, length us, event | category | flops | bytes accessed | tf_op | source)
XLA Modules:
  0.0 102.6 jit_solution(13708597530030498742)
XLA Ops:
  0.6 99.6 %shard_map.173 = (bf16[1,2048]{1,0:T(2,128)(2,1)S(1)}, bf16[3,64,4096]{2,1,0:T(8,128)(2,1)S(1)}, bf16[3,64,4096]{2,1,0:T(8,128)(2,1)S(1)}, bf16[64,8192]{1,0:T(8,128)(2,1)S(1)}, bf16[64,8192]{1,0:T(8,128)(2,1)S(1)}) custom-call(s32[8]{0:T(128)} %len_in.1, bf16[1,2048]{1,0:T(2,128)(2,1)} %hid_in.1, bf16[4,2048]{1,0:T(4,128)(2,1)} %gain_in.1, ...), custom_call_target="tpu_custom_call" | custom-call | tf_op jit(solution)/shard_map/pallas_call | solution.py:396
  100.2 2.4 %shard_map.174 = (bf16[1,2048]{1,0:T(2,128)(2,1)}, bf16[3,64,4096]{2,1,0:T(8,128)(2,1)}, bf16[3,64,4096]{2,1,0:T(8,128)(2,1)}, bf16[64,8192]{1,0:T(8,128)(2,1)}, bf16[64,8192]{1,0:T(8,128)(2,1)}) custom-call(bf16[1,2048]{1,0:T(2,128)(2,1)S(1)} %get-tuple-element.15.refs_0_, bf16[3,64,4096]{2,1,0:T(8,128)(2,1)S(1)} %get-tuple-element.16.refs_1_, ...), custom_call_target="tpu_custom_call" | custom-call | tf_op jit(solution)/shard_map/pallas_call | solution.py:442

commit v4 on v3

--- a/solution.py
+++ b/solution.py
@@ -157,16 +157,28 @@
     residual = jnp.concatenate([hid_ref[0:1, b * LANES:(b + 1) * LANES] for b in range(blocks)], axis=0)
 
     lane_t = lax.broadcasted_iota(jnp.int32, (SUBLANES, LANES), 1)
+    sublane_t = lax.broadcasted_iota(jnp.int32, (SUBLANES, LANES), 0)
+    middle = SUBLANES * n_sp
     all_messages = []
 
-    def attention_query(layer, sliding):
+    def attention_query(sliding):
         q = query[...]
         if sliding:
             partner = jnp.where(first_half, pltpu.roll(q, q_width - half, 1), pltpu.roll(q, half, 1))
             q = q * cos_row + jnp.where(first_half, -partner, partner) * sin_row
+        return q.astype(BF16).astype(F32)
+
+    def split_heads(q):
         q = jnp.where(own_head, q, 0.0)
         q = functools.reduce(lambda a, b: a + b, [q[:, b * LANES:(b + 1) * LANES] for b in range(q_width // LANES)])
-        return (q + pltpu.roll(q, head_dim, 1)).astype(BF16)
+        return (q[:, :head_dim] + q[:, head_dim:2 * head_dim]).astype(BF16)
+
+    def flat_heads(heads):
+        spread = jnp.where(own_head, jnp.concatenate([heads] * n_heads, axis=1), 0.0)
+        return jnp.sum(spread, axis=0, keepdims=True)
+
+    def flat_lanes(row, first):
+        return lane_t == first + n_sp * sublane_t + row
 
     def pieces(layer, kv, columns):
         sliding = layer < n_layers - 1
@@ -203,22 +215,21 @@
         local_copies[0].wait()
         positions = me * piece + lax.broadcasted_iota(jnp.int32, (SUBLANES, piece), 1)
         new_score = jnp.dot(q_heads, jnp.broadcast_to(k_new, (head_dim, LANES)), preferred_element_type=F32) * head_dim ** -0.5
-        tops = jnp.zeros((SUBLANES, LANES), F32)
-        norms = jnp.zeros((SUBLANES, LANES), F32)
+        packed = jnp.zeros((SUBLANES, LANES), F32)
         for row in range(n_sp):
-            score = jnp.dot(queries[row][:, :head_dim].astype(BF16), local[0, row], preferred_element_type=F32) * head_dim ** -0.5
+            row_heads = split_heads(jnp.broadcast_to(queries[row], (SUBLANES, q_width)))
+            score = jnp.dot(row_heads, local[0, row], preferred_element_type=F32) * head_dim ** -0.5
             valid = (positions > len_ref[row] - WINDOW) & (positions < len_ref[row])
             score = jnp.where(valid, score, -1e30)
             local_score[row] = score
             top = jnp.max(score, axis=1, keepdims=True)
             norm = jnp.sum(jnp.exp(score - top), axis=1, keepdims=True)
-            tops = jnp.where(lane_t == row, top, tops)
-            norms = jnp.where(lane_t == row, norm, norms)
-        mine = lane_t == me
-        raised = jnp.where(mine, jnp.maximum(tops, new_score), tops)
-        norms = jnp.where(mine, norms * jnp.exp(tops - raised) + jnp.exp(jnp.where(mine, new_score - raised, 0.0)), norms)
-        stats[me, 0] = raised
-        stats[me, 1] = norms
+            mine = me == row
+            raised = jnp.where(mine, jnp.maximum(top, new_score[:, 0:1]), top)
+            norm = norm * jnp.exp(top - raised) + jnp.where(mine, jnp.exp(jnp.minimum(new_score[:, 0:1] - raised, 0.0)), 0.0)
+            packed = jnp.where(flat_lanes(row, 0), raised, packed)
+            packed = jnp.where(flat_lanes(row, middle), norm, packed)
+        stats[me] = jnp.sum(packed, axis=0, keepdims=True)
         sent = messages(1, lambda dst: stats.at[me], stats.at[me])
         all_messages.extend(sent)
         start_bulk(*bulk_order[2])
@@ -227,25 +238,28 @@
         for copy in sent:
             copy.wait_recv()
         local_copies[1].wait()
-        top = functools.reduce(jnp.maximum, [stats[src, 0] for src in range(n_sp)])
-        norm = functools.reduce(jnp.add, [stats[src, 1] * jnp.exp(stats[src, 0] - top) for src in range(n_sp)])
-        share = 1.0 / jnp.where(lane_t < n_sp, norm, 1.0)
+        gathered = [jnp.broadcast_to(stats[src], (SUBLANES, LANES)) for src in range(n_sp)]
+        low = lane_t < middle
+        top = functools.reduce(jnp.maximum, gathered)
+        norm = functools.reduce(jnp.add, [pltpu.roll(each, LANES - middle, 1) * jnp.exp(jnp.where(low, each - top, 0.0)) for each in gathered])
+        share = 1.0 / jnp.where(low, norm, 1.0)
+
+        def column(tile, row):
+            return jnp.sum(jnp.where(flat_lanes(row, 0), tile, 0.0), axis=1, keepdims=True)
+
         for row in range(n_sp):
-            weight = (jnp.exp(local_score[row] - top[:, row:row + 1]) * share[:, row:row + 1]).astype(BF16)
-            partial = contract_lanes(weight, local[1, row])
-            values_out[row] = jnp.concatenate([partial, partial], axis=1)
+            weight = (jnp.exp(local_score[row] - column(top, row)) * column(share, row)).astype(BF16)
+            values_out[row] = flat_heads(contract_lanes(weight, local[1, row]))
         sent = messages(2, lambda dst: values_out.at[dst], values_in.at[me])
         all_messages.extend(sent)
         for group in bulk_order[3:]:
             start_bulk(*group)
-        my_top = jnp.sum(jnp.where(mine, top, 0.0), axis=1, keepdims=True)
-        my_share = jnp.sum(jnp.where(mine, share, 0.0), axis=1, keepdims=True)
-        new_weight = (jnp.exp(new_score[:, 0:1] - my_top) * my_share).astype(BF16).astype(F32)
-        mixed = new_weight * v_row + values_out[me][:, :head_dim]
+        new_weight = (jnp.exp(new_score[:, 0:1] - column(top, me)) * column(share, me)).astype(BF16).astype(F32)
+        mixed = flat_heads(new_weight * v_row) + values_out[me]
         for copy in sent:
             copy.wait_recv()
         for step in range(1, n_sp):
-            mixed = mixed + values_in[lax.rem(me + step, n_sp)][:, :head_dim]
+            mixed = mixed + values_in[lax.rem(me + step, n_sp)]
         return mixed
 
     for layer in range(n_layers):
@@ -268,10 +282,10 @@
             cols = pl.ds(pl.multiple_of(n * TILE, TILE), TILE)
             query[:, cols] = jnp.dot(normed[...], wq[slot, :, cols], preferred_element_type=F32)
 
-        q_wide = attention_query(layer, sliding)
-        q_heads = q_wide[:, :head_dim]
+        q_wide = attention_query(sliding)
+        q_heads = split_heads(q_wide)
         if layer == 0:
-            queries[me] = q_wide.astype(F32)
+            queries[me] = q_wide[0:1]
             sent = messages(0, lambda dst: queries.at[me], queries.at[me])
             all_messages.extend(sent)
             start_bulk(*bulk_order[1])
@@ -323,9 +337,8 @@
             scores = [jnp.exp(score - top) for score in scores]
             share = 1.0 / functools.reduce(jnp.add, [jnp.sum(score, axis=1, keepdims=True) for score in scores])
             weights = [(score * share).astype(BF16) for score in scores]
-            mixed = functools.reduce(jnp.add, [contract_lanes(weight, values) for weight, (part, values) in zip(weights, pieces(layer, 1, columns))])
-        mixed = jnp.where(own_head, jnp.concatenate([mixed] * n_heads, axis=1), 0.0)
-        mixed = jnp.broadcast_to(jnp.sum(mixed, axis=0, keepdims=True), mixed.shape).astype(BF16)
+            mixed = flat_heads(functools.reduce(jnp.add, [contract_lanes(weight, values) for weight, (part, values) in zip(weights, pieces(layer, 1, columns))]))
+        mixed = jnp.broadcast_to(mixed, (SUBLANES, q_width)).astype(BF16)
         waits[6].wait()
         for n in range(dim // TILE):
             attn = jnp.dot(mixed, wo[slot, :, n * TILE:(n + 1) * TILE], preferred_element_type=F32)
@@ -419,10 +432,10 @@
                 pltpu.VMEM(freq_col.shape, F32),
                 pltpu.VMEM((2, n_rows, head_dim, piece), BF16),
                 pltpu.VMEM((n_rows, SUBLANES, piece), F32),
-                pltpu.VMEM((n_sp, SUBLANES, LANES), F32),
-                pltpu.VMEM((n_sp, 2, SUBLANES, LANES), F32),
-                pltpu.VMEM((n_sp, SUBLANES, LANES), F32),
-                pltpu.VMEM((n_sp, SUBLANES, LANES), F32),
+                pltpu.VMEM((n_sp, 1, q_width), F32),
+                pltpu.VMEM((n_sp, 1, LANES), F32),
+                pltpu.VMEM((n_sp, 1, q_width), F32),
+                pltpu.VMEM((n_sp, 1, q_width), F32),
                 pltpu.SemaphoreType.DMA((n_layers, 2, n_sp)),
                 pltpu.SemaphoreType.DMA((n_layers, 2, n_sp)),
                 pltpu.SemaphoreType.DMA((n_layers, 2)),

time: 103 us -> 102 us (level)
  no operation moved by 1% of the time
where the time goes in v4:
time: 102 us
  Pallas kernels  101 us (99%)
    pallas_call x1, Pallas kernels, device_step(): pl.pallas_call(functools.partial(decode_kernel, n_sp, n_tp), out_shape=[p...  98.6 us
    pallas_call x1, Pallas kernels, device_step(): pl.pallas_call(write_kernel, out_shape=[jax.ShapeDtypeStruct(shape, BF16)...  2.4 us

profile of v4, /device:TPU:97, one launch (start us, length us, event | category | flops | bytes accessed | tf_op | source)
XLA Modules:
  0.0 101.7 jit_solution(15661140492930765008)
XLA Ops:
  0.6 98.6 %shard_map.173 = (bf16[1,2048]{1,0:T(2,128)(2,1)S(1)}, bf16[3,64,4096]{2,1,0:T(8,128)(2,1)S(1)}, bf16[3,64,4096]{2,1,0:T(8,128)(2,1)S(1)}, bf16[64,8192]{1,0:T(8,128)(2,1)S(1)}, bf16[64,8192]{1,0:T(8,128)(2,1)S(1)}) custom-call(s32[8]{0:T(128)} %len_in.1, bf16[1,2048]{1,0:T(2,128)(2,1)} %hid_in.1, bf16[4,2048]{1,0:T(4,128)(2,1)} %gain_in.1, ...), custom_call_target="tpu_custom_call" | custom-call | tf_op jit(solution)/shard_map/pallas_call | solution.py:409
  99.3 2.4 %shard_map.174 = (bf16[1,2048]{1,0:T(2,128)(2,1)}, bf16[3,64,4096]{2,1,0:T(8,128)(2,1)}, bf16[3,64,4096]{2,1,0:T(8,128)(2,1)}, bf16[64,8192]{1,0:T(8,128)(2,1)}, bf16[64,8192]{1,0:T(8,128)(2,1)}) custom-call(bf16[1,2048]{1,0:T(2,128)(2,1)S(1)} %get-tuple-element.15.refs_0_, bf16[3,64,4096]{2,1,0:T(8,128)(2,1)S(1)} %get-tuple-element.16.refs_1_, ...), custom_call_target="tpu_custom_call" | custom-call | tf_op jit(solution)/shard_map/pallas_call | solution.py:455
